TPU v7x, 64 devices: a 2x2x8 block of a 4x4x8 slice. The times are simulated.
64 devices in a mesh: dp: 8 (over x, y, core), tp: 8 (over z).
Axes of the slice: x: 2, y: 2, z: 8, core: 2. Of those that a mesh axis runs over, the one named last changes fastest.
The devices are a block of a 4x4x8 slice.
Arguments:
- x: bfloat16 [1024, 12288], P('dp'), parts along dimension 0
- w_gate: bfloat16 [12288, 33792], P(None, 'tp')
- w_up: bfloat16 [12288, 33792], P(None, 'tp')
- w_down: bfloat16 [33792, 12288], P('tp')
Outputs:
- output: bfloat16 [1024, 12288], P('dp'), parts along dimension 0
There are 8 independent parts. A program takes and returns all parts, laid end to end along the dimension named above; an argument that names none is the same for every part.
All inputs are finite; a program needn't handle non-finite values.
Results may differ from a plain program's by a relative error of at most 0.016.
Values are sent between devices in bfloat16 or wider.
A program may use at most 768 MiB of HBM per device.

v0:
```python
import jax
import jax.numpy as jnp
from jax import lax
from jax.sharding import PartitionSpec as P


def solution(mesh):
    def step(x, w_gate, w_up, w_down):
        gate = jnp.dot(x, w_gate, preferred_element_type=jnp.float32)
        up = jnp.dot(x, w_up, preferred_element_type=jnp.float32)
        hidden = (jax.nn.silu(gate) * up).astype(jnp.bfloat16)
        term = jnp.dot(hidden, w_down, preferred_element_type=jnp.float32).astype(jnp.bfloat16)
        return lax.psum(term, "tp")

    return jax.shard_map(
        step,
        mesh=mesh,
        in_specs=(P("dp", None), P(None, "tp"), P(None, "tp"), P("tp", None)),
        out_specs=P("dp", None),
        check_vma=False,
    )
```

profile of v0, /device:TPU:21, one launch (start us, length us, event | category | flops | bytes accessed | tf_op | source)
XLA Modules:
  0.0 215.6 jit_solution(2860991191767395881)
XLA Ops:
  6.5 0.0 copy-start
  6.6 0.0 all-reduce.2.cloned.1.call-start
  6.6 1.9 copy-done
  8.4 35.8 %fusion.1 = f32[128,4224]{1,0:T(8,128)} fusion(bf16[128,12288]{1,0:T(8,128)(2,1)S(1)} %copy-done, bf16[12288,4224]{1,0:T(8,128)(2,1)} %param.5), kind=kOutput, calls=%fused_computation.3 | convolution fusion | flops 13287555072 | bytes 109117440 | tf_op jit(solution)/shard_map/dot_general | solution.py:9
  44.3 35.6 %fusion = bf16[128,4224]{1,0:T(8,128)(2,1)} fusion(bf16[128,12288]{1,0:T(8,128)(2,1)S(1)} %copy-done, bf16[12288,4224]{1,0:T(8,128)(2,1)} %param.6, f32[128,4224]{1,0:T(8,128)} %fusion.1), kind=kOutput, calls=%fused_computation.2 | convolution fusion | flops 13290799104 | bytes 110198784 | tf_op jit(solution)/shard_map/dot_general | solution.py:10
  79.9 36.4 %convolution_convert_fusion = bf16[128,12288]{1,0:T(8,128)(2,1)} fusion(bf16[128,4224]{1,0:T(8,128)(2,1)} %fusion, bf16[4224,12288]{1,0:T(8,128)(2,1)} %param.7), kind=kOutput, calls=%fused_computation | convolution fusion | flops 13289127936 | bytes 108036096 | tf_op jit(solution)/shard_map/dot_general | solution.py:12
  116.3 0.1 all-reduce.2.cloned.1.call-update
  116.4 88.5 %all-reduce.2.cloned.1.call-done = bf16[128,12288]{1,0:T(8,128)(2,1)} async-done(((bf16[128,12288]{1,0:T(8,128)(2,1)}), bf16[128,12288]{1,0:T(8,128)(2,1)}) %all-reduce.2.cloned.1.call-update) | async-done | bytes 3145744 | tf_op jit(solution)/shard_map/psum | solution.py:13
  204.9 3.8 %copy.6 = bf16[128,12288]{1,0:T(8,128)(2,1)} copy(bf16[128,12288]{1,0:T(8,128)(2,1)} %all-reduce.2.cloned.1.call-done) | data formatting | bytes 6291456
Async XLA Ops:
  6.5 1.9 copy-start
  6.6 198.3 %all-reduce.2.cloned.1.call-start = ((), (), s32[]{:S(2)}) async-start(), calls=%async_computation | async-start | bytes 6291456 | tf_op jit(solution)/shard_map/psum | solution.py:13
Sparse Core Ops, SparseCore 0:
  116.5 88.3 all-reduce.1
where the time goes:
time: 216 us
  matrix products  108 us (50%)
  waiting for transfers between devices  88.6 us (41%)
  between operations  13.4 us (6%)
  local copies, waits for them, and re-layouts  5.72 us (3%)
    psum x1, waiting for transfers between devices, step(): return lax.psum(term, 'tp')  88.5 us
    dot_general x1, matrix products, step(): jnp.dot(hidden, w_down, preferred_element_type=jnp.float32)  36.4 us
    dot_general x1, matrix products, step(): gate = jnp.dot(x, w_gate, preferred_element_type=jnp.float32)  35.8 us
    dot_general x1, matrix products, step(): up = jnp.dot(x, w_up, preferred_element_type=jnp.float32)  35.6 us
    unnamed x3, local copies, waits for them, and re-layouts  5.72 us
  transfers between devices with their start and end apart: 1, of which 1 were waited for; matrix products, arithmetic and copies ran while one was open for 0% of the time, Pallas kernels for 0%

commit v1 on v0

v1 whole, which is shorter than its diff:
```python
import functools

import jax
import jax.numpy as jnp
from jax import lax
from jax.experimental import pallas as pl
from jax.experimental.pallas import tpu as pltpu
from jax.sharding import PartitionSpec as P

LANES = 128
SUBS = 3
SLABS = 16
SLAB_SLOTS = 3
DOWN_SLOTS = 4
MESH = pl.DeviceIdType.MESH
VMEM_BYTES = 67_043_328


def kernel(n, x_hbm, wg_hbm, wu_hbm, wd_hbm, y_hbm, xall, acc, hid, wbuf, dbuf, term, psend, precv,
           rsend, rrecv, ybuf, x_own_sem, x_send_sem, x_recv_sem, w_sem, d_sem, p_send_sem,
           p_recv_sem, r_send_sem, r_recv_sem, g_send_sem, g_recv_sem, y_sem):
    dp, tp = lax.axis_index("dp"), lax.axis_index("tp")
    half = lax.rem(dp, 2)
    partner = {"dp": dp + 1 - 2 * half}
    neighbour = ({"tp": lax.rem(tp + 1, n)}, {"tp": lax.rem(tp + n - 1, n)})

    rows, depth = x_hbm.shape
    slabs, _, slab = xall.shape
    width = hid.shape[1]
    local = wd_hbm.shape[0]
    first = pl.multiple_of(half * (local - width), LANES)
    overlap = 2 * width - local
    sub = ybuf.shape[1] // (2 * n * SUBS)
    chunk = sub * SUBS
    pairs = n * SUBS

    def weights(i, slot, act=lambda c: c.start()):
        k = pl.multiple_of(i * slab, LANES)
        for j, w in enumerate((wg_hbm, wu_hbm)):
            act(pltpu.make_async_copy(
                w.at[pl.ds(k, slab), pl.ds(first, width)],
                wbuf.at[slot, :, pl.ds(j * width, width)],
                w_sem.at[slot, j],
            ))

    def column(d, j, u):
        return pl.multiple_of((d * n + j) * chunk + u * sub, LANES)

    def ring_chunk(s, d):
        return lax.rem(tp + n - s, n) if d == 0 else lax.rem(tp + s, n)

    def down(s, u, act=lambda c: c.start()):
        slot = lax.rem(s * SUBS + u, DOWN_SLOTS)
        for d in range(2):
            act(pltpu.make_async_copy(
                wd_hbm.at[pl.ds(first, width), pl.ds(column(d, ring_chunk(s, d), u), sub)],
                dbuf.at[slot, :, pl.ds(d * sub, sub)],
                d_sem.at[slot, d],
            ))

    def own_copy(i):
        k = pl.multiple_of(i * slab, LANES)
        return pltpu.make_async_copy(
            x_hbm.at[:, pl.ds(k, slab)], xall.at[i, pl.ds(0, rows)], x_own_sem.at[i])

    def partner_copy(i):
        k = pl.multiple_of(i * slab, LANES)
        return pltpu.make_async_remote_copy(
            src_ref=x_hbm.at[:, pl.ds(k, slab)], dst_ref=xall.at[i, pl.ds(rows, rows)],
            send_sem=x_send_sem.at[i], recv_sem=x_recv_sem.at[i],
            device_id=partner, device_id_type=MESH)

    def term_copy(q):
        return pltpu.make_async_remote_copy(
            src_ref=psend.at[q], dst_ref=precv.at[q],
            send_sem=p_send_sem.at[q], recv_sem=p_recv_sem.at[q],
            device_id=partner, device_id_type=MESH)

    def ring_copy(s, u, d):
        i = s * SUBS + u
        return pltpu.make_async_remote_copy(
            src_ref=rsend.at[i, d], dst_ref=rrecv.at[i, d],
            send_sem=r_send_sem.at[i, d], recv_sem=r_recv_sem.at[i, d],
            device_id=neighbour[d], device_id_type=MESH)

    def gather_copy(a, u, d):
        j = ring_chunk(a - 1, d) if not (isinstance(a, int) and a == 0) else ring_chunk(n - 1, d)
        col = pl.ds(column(d, j, u), sub)
        i = a * SUBS + u
        return pltpu.make_async_remote_copy(
            src_ref=ybuf.at[:, col], dst_ref=ybuf.at[:, col],
            send_sem=g_send_sem.at[i, d], recv_sem=g_recv_sem.at[i, d],
            device_id=neighbour[d], device_id_type=MESH)

    def out_copy(a, u, d):
        j = ring_chunk(a, d) if a < n - 1 else ring_chunk(n - 1, d)
        col = pl.ds(column(d, j, u), sub)
        return pltpu.make_async_copy(ybuf.at[:, col], y_hbm.at[:, col], y_sem.at[a * SUBS + u, d])

    for i in range(slabs):
        own_copy(i).start()
        if i < SLAB_SLOTS:
            weights(i, i)
    barrier = pltpu.get_barrier_semaphore()
    for other in (partner,) + neighbour:
        pl.semaphore_signal(barrier, inc=1, device_id=other, device_id_type=MESH)
    pl.semaphore_wait(barrier, 3)
    for i in range(slabs):
        partner_copy(i).start()
    acc[...] = jnp.zeros_like(acc)

    def slab_ready(i, slot):
        own_copy(i).wait()
        partner_copy(i).wait_recv()
        weights(i, slot, lambda c: c.wait())

    @pl.loop(0, slabs - 1)
    def _(i):
        slot = lax.rem(i, SLAB_SLOTS)
        slab_ready(i, slot)
        acc[...] += jnp.dot(xall[i], wbuf[slot], preferred_element_type=jnp.float32)

        @pl.when(i + SLAB_SLOTS < slabs)
        def _():
            weights(i + SLAB_SLOTS, slot)

        @pl.when(i + SLAB_SLOTS == slabs - 1)
        def _():
            for q in range(DOWN_SLOTS):
                down(q // SUBS, q % SUBS)

    last = slabs - 1
    slot = last % SLAB_SLOTS
    slab_ready(last, slot)
    for c in range(0, width, 2 * LANES):
        w = min(2 * LANES, width - c)
        gate, up = (
            acc[:, c + o:c + o + w]
            + jnp.dot(xall[last], wbuf[slot, :, c + o:c + o + w], preferred_element_type=jnp.float32)
            for o in (0, width)
        )
        h = gate * jax.nn.sigmoid(gate) * up
        if c < overlap:
            unit = lax.broadcasted_iota(jnp.int32, h.shape, 1) + c
            h = jnp.where(unit < overlap * half, 0.0, h)
        hid[:, c:c + w] = h.astype(jnp.bfloat16)

    def matmul(s, u, more):
        q = s * SUBS + u
        slot = lax.rem(q, DOWN_SLOTS)
        down(s, u, lambda c: c.wait())
        t = jnp.dot(hid[...], dbuf[slot], preferred_element_type=jnp.float32)
        psend[q] = t[rows:].astype(jnp.bfloat16)
        term_copy(q).start()
        term[q] = t[:rows]
        if more:
            later = q + DOWN_SLOTS
            down(later // SUBS, lax.rem(later, SUBS))

    def pass_on(s, u):
        q = s * SUBS + u
        term_copy(q).wait_recv()
        start = isinstance(s, int) and s == 0
        end = isinstance(s, int) and s == n - 1
        for d in range(2):
            cut = slice(d * sub, (d + 1) * sub)
            v = term[q, :, cut] + precv[q, :, cut].astype(jnp.float32)
            if not start:
                ring_copy(s - 1, u, d).wait_recv()
                v = v + rrecv[(s - 1) * SUBS + u, d].astype(jnp.float32)
            v = v.astype(jnp.bfloat16)
            if end:
                ybuf[:, pl.ds(column(d, ring_chunk(n - 1, d), u), sub)] = v
                gather_copy(0, u, d).start()
                out_copy(n - 1, u, d).start()
            else:
                rsend[q, d] = v
                ring_copy(s, u, d).start()

    def step(s, behind):
        for u in range(SUBS):
            q = s * SUBS + u
            matmul(s, u, not isinstance(s, int) or q + DOWN_SLOTS < pairs)
            if u >= behind:
                pass_on(s, u - behind)
            elif not (isinstance(s, int) and s == 0):
                pass_on(s - 1, u - behind + SUBS)

    BEHIND = 2
    step(0, BEHIND)
    step(1, BEHIND)
    full = (pairs - DOWN_SLOTS) // SUBS

    @pl.loop(2, full)
    def _(s):
        step(s, BEHIND)

    for s in range(full, n):
        step(s, BEHIND)
    for u in range(SUBS - BEHIND, SUBS):
        pass_on(n - 1, u)

    for a in range(n - 1):
        for u in range(SUBS):
            for d in range(2):
                gather_copy(a, u, d).wait_recv()
                if a + 1 < n - 1:
                    gather_copy(a + 1, u, d).start()
                out_copy(a, u, d).start()

    for i in range(slabs):
        partner_copy(i).wait_send()
    for q in range(pairs):
        term_copy(q).wait_send()
    for a in range(n):
        for u in range(SUBS):
            for d in range(2):
                if a < n - 1:
                    ring_copy(a, u, d).wait_send()
                    gather_copy(a, u, d).wait_send()
                out_copy(a, u, d).wait()


def block(n, x, w_gate, w_up, w_down):
    rows, depth = x.shape
    local = w_down.shape[0]
    blocks = local // LANES
    width = (blocks + 1) // 2 * LANES
    slab = depth // SLABS
    sub = depth // (2 * n * SUBS)
    pairs = n * SUBS
    bf16, f32 = jnp.bfloat16, jnp.float32
    dma = pltpu.SemaphoreType.DMA
    return pl.pallas_call(
        functools.partial(kernel, n),
        out_shape=jax.ShapeDtypeStruct((rows, depth), bf16),
        in_specs=[pl.BlockSpec(memory_space=pl.ANY)] * 4,
        out_specs=pl.BlockSpec(memory_space=pl.ANY),
        scratch_shapes=[
            pltpu.VMEM((SLABS, 2 * rows, slab), bf16),
            pltpu.VMEM((2 * rows, 2 * width), f32),
            pltpu.VMEM((2 * rows, width), bf16),
            pltpu.VMEM((SLAB_SLOTS, slab, 2 * width), bf16),
            pltpu.VMEM((DOWN_SLOTS, width, 2 * sub), bf16),
            pltpu.VMEM((pairs, rows, 2 * sub), f32),
            pltpu.VMEM((pairs, rows, 2 * sub), bf16),
            pltpu.VMEM((pairs, rows, 2 * sub), bf16),
            pltpu.VMEM((pairs - SUBS, 2, rows, sub), bf16),
            pltpu.VMEM((pairs - SUBS, 2, rows, sub), bf16),
            pltpu.VMEM((rows, depth), bf16),
            dma((SLABS,)), dma((SLABS,)), dma((SLABS,)),
            dma((SLAB_SLOTS, 2)), dma((DOWN_SLOTS, 2)),
            dma((pairs,)), dma((pairs,)),
            dma((pairs - SUBS, 2)), dma((pairs - SUBS, 2)),
            dma((pairs - SUBS, 2)), dma((pairs - SUBS, 2)),
            dma((pairs, 2)),
        ],
        compiler_params=pltpu.CompilerParams(
            collective_id=0, has_side_effects=True, vmem_limit_bytes=VMEM_BYTES),
        name="mlp",
    )(x, w_gate, w_up, w_down)


def solution(mesh):
    n = mesh.shape["tp"]
    return jax.shard_map(
        functools.partial(block, n),
        mesh=mesh,
        in_specs=(P("dp", None), P(None, "tp"), P(None, "tp"), P("tp", None)),
        out_specs=P("dp", None),
        check_vma=False,
    )
```

time: 216 us -> 115 us (0.53)
  Pallas kernels: 0 us -> 111 us
  matrix products: 108 us -> 0 us
  waiting for transfers between devices: 88.6 us -> 0 us
  between operations: 13.4 us -> 0.01 us
    pallas_call x0 -> x1, Pallas kernels: none -> 111 us  [block(): pl.pallas_call(functools.partial(kernel, n), out_shape=jax.ShapeDtypeStru...]
    dot_general x3 -> x0, matrix products: 108 us -> none  [the longest x1 36.4 us: step(): jnp.dot(hidden, w_down, preferred_element_type=jnp.float32)]
    psum x1 -> x0, waiting for transfers between devices: 88.5 us -> none  [step(): return lax.psum(term, 'tp')]
    unnamed x3 -> x1, local copies, waits for them, and re-layouts: 5.72 us -> 3.83 us
  transfers between devices with their start and end apart: 1 -> 0, of which waited for: 1 -> 0; matrix products, arithmetic and copies ran while one was open for 0% -> 0% of each run, Pallas kernels for 0% -> 0%
where the time goes in v1:
time: 115 us
  Pallas kernels  111 us (97%)
  local copies, waits for them, and re-layouts  3.83 us (3%)
    pallas_call x1, Pallas kernels, block(): pl.pallas_call(functools.partial(kernel, n), out_shape=jax.ShapeDtypeStru...  111 us
    unnamed x1, local copies, waits for them, and re-layouts  3.83 us

profile of v1, /device:TPU:21, one launch (start us, length us, event | category | flops | bytes accessed | tf_op | source)
XLA Modules:
  0.0 114.6 jit_solution(3469990692621221968)
XLA Ops:
  0.0 110.8 %mlp.1 = bf16[128,12288]{1,0:T(8,128)(2,1)} custom-call(bf16[128,12288]{1,0:T(8,128)(2,1)} %x_hbm.1, bf16[12288,4224]{1,0:T(8,128)(2,1)} %wg_hbm.1, bf16[12288,4224]{1,0:T(8,128)(2,1)} %wu_hbm.1, bf16[4224,12288]{1,0:T(8,128)(2,1)} %wd_hbm.1), custom_call_target="tpu_custom_call" | custom-call | tf_op jit(solution)/shard_map/mlp/pallas_call | solution.py:234
  110.8 3.8 %copy.6 = bf16[128,12288]{1,0:T(8,128)(2,1)} copy(bf16[128,12288]{1,0:T(8,128)(2,1)} %mlp.1) | data formatting | bytes 6291456

commit v2 on v1

--- a/solution.py
+++ b/solution.py
@@ -9,16 +9,18 @@
 
 LANES = 128
 SUBS = 3
+HALVES = 2
+PARTS = 3
 SLABS = 16
 SLAB_SLOTS = 3
-DOWN_SLOTS = 4
+DOWN_SLOTS = 3
 MESH = pl.DeviceIdType.MESH
-VMEM_BYTES = 67_043_328
-
-
-def kernel(n, x_hbm, wg_hbm, wu_hbm, wd_hbm, y_hbm, xall, acc, hid, wbuf, dbuf, term, psend, precv,
-           rsend, rrecv, ybuf, x_own_sem, x_send_sem, x_recv_sem, w_sem, d_sem, p_send_sem,
-           p_recv_sem, r_send_sem, r_recv_sem, g_send_sem, g_recv_sem, y_sem):
+VMEM_BYTES = 62_000_000
+
+
+def kernel(n, x_hbm, wg_hbm, wu_hbm, wd_hbm, ybuf, xall, acc, hid, wbuf, dbuf, term, psend, precv,
+           rsend, rrecv, x_own_sem, x_send_sem, x_recv_sem, w_sem, l_sem, d_sem, p_send_sem,
+           p_recv_sem, r_send_sem, r_recv_sem, g_send_sem, g_recv_sem):
     dp, tp = lax.axis_index("dp"), lax.axis_index("tp")
     half = lax.rem(dp, 2)
     partner = {"dp": dp + 1 - 2 * half}
@@ -30,9 +32,14 @@
     local = wd_hbm.shape[0]
     first = pl.multiple_of(half * (local - width), LANES)
     overlap = 2 * width - local
-    sub = ybuf.shape[1] // (2 * n * SUBS)
+    sub = depth // (2 * n * SUBS)
     chunk = sub * SUBS
     pairs = n * SUBS
+    pieces = SUBS * HALVES
+    piece = sub // HALVES
+    last = slabs - 1
+    cuts = [c * 2 * LANES for c in range(-(-width // (2 * LANES)))]
+    parts = [cuts[p * len(cuts) // PARTS] for p in range(PARTS)] + [width]
 
     def weights(i, slot, act=lambda c: c.start()):
         k = pl.multiple_of(i * slab, LANES)
@@ -43,6 +50,15 @@
                 w_sem.at[slot, j],
             ))
 
+    def last_weights(p, act=lambda c: c.start()):
+        a, b = parts[p], parts[p + 1]
+        for j, w in enumerate((wg_hbm, wu_hbm)):
+            act(pltpu.make_async_copy(
+                w.at[pl.ds(last * slab, slab), pl.ds(pl.multiple_of(first + a, LANES), b - a)],
+                wbuf.at[last % SLAB_SLOTS, :, pl.ds(j * width + a, b - a)],
+                l_sem.at[p, j],
+            ))
+
     def column(d, j, u):
         return pl.multiple_of((d * n + j) * chunk + u * sub, LANES)
 
@@ -76,26 +92,23 @@
             send_sem=p_send_sem.at[q], recv_sem=p_recv_sem.at[q],
             device_id=partner, device_id_type=MESH)
 
-    def ring_copy(s, u, d):
-        i = s * SUBS + u
+    def ring_copy(s, p, d):
+        i = s * pieces + p
         return pltpu.make_async_remote_copy(
             src_ref=rsend.at[i, d], dst_ref=rrecv.at[i, d],
             send_sem=r_send_sem.at[i, d], recv_sem=r_recv_sem.at[i, d],
             device_id=neighbour[d], device_id_type=MESH)
 
-    def gather_copy(a, u, d):
-        j = ring_chunk(a - 1, d) if not (isinstance(a, int) and a == 0) else ring_chunk(n - 1, d)
-        col = pl.ds(column(d, j, u), sub)
-        i = a * SUBS + u
+    def place(j, p, d):
+        return (d * n + j) * pieces + p
+
+    def gather_copy(a, p, d):
+        at = place(ring_chunk(n - 1 if a == 0 else a - 1, d), p, d)
+        i = a * pieces + p
         return pltpu.make_async_remote_copy(
-            src_ref=ybuf.at[:, col], dst_ref=ybuf.at[:, col],
+            src_ref=ybuf.at[at], dst_ref=ybuf.at[at],
             send_sem=g_send_sem.at[i, d], recv_sem=g_recv_sem.at[i, d],
             device_id=neighbour[d], device_id_type=MESH)
-
-    def out_copy(a, u, d):
-        j = ring_chunk(a, d) if a < n - 1 else ring_chunk(n - 1, d)
-        col = pl.ds(column(d, j, u), sub)
-        return pltpu.make_async_copy(ybuf.at[:, col], y_hbm.at[:, col], y_sem.at[a * SUBS + u, d])
 
     for i in range(slabs):
         own_copy(i).start()
@@ -109,30 +122,33 @@
         partner_copy(i).start()
     acc[...] = jnp.zeros_like(acc)
 
-    def slab_ready(i, slot):
+    def rows_ready(i):
         own_copy(i).wait()
         partner_copy(i).wait_recv()
-        weights(i, slot, lambda c: c.wait())
 
     @pl.loop(0, slabs - 1)
     def _(i):
         slot = lax.rem(i, SLAB_SLOTS)
-        slab_ready(i, slot)
+        rows_ready(i)
+        weights(i, slot, lambda c: c.wait())
         acc[...] += jnp.dot(xall[i], wbuf[slot], preferred_element_type=jnp.float32)
 
-        @pl.when(i + SLAB_SLOTS < slabs)
+        @pl.when(i + SLAB_SLOTS < last)
         def _():
             weights(i + SLAB_SLOTS, slot)
 
-        @pl.when(i + SLAB_SLOTS == slabs - 1)
+        @pl.when(i + SLAB_SLOTS == last)
         def _():
+            for p in range(PARTS):
+                last_weights(p)
             for q in range(DOWN_SLOTS):
                 down(q // SUBS, q % SUBS)
 
-    last = slabs - 1
     slot = last % SLAB_SLOTS
-    slab_ready(last, slot)
-    for c in range(0, width, 2 * LANES):
+    rows_ready(last)
+    for c in cuts:
+        if c in parts:
+            last_weights(parts.index(c), lambda c: c.wait())
         w = min(2 * LANES, width - c)
         gate, up = (
             acc[:, c + o:c + o + w]
@@ -162,20 +178,21 @@
         term_copy(q).wait_recv()
         start = isinstance(s, int) and s == 0
         end = isinstance(s, int) and s == n - 1
-        for d in range(2):
-            cut = slice(d * sub, (d + 1) * sub)
-            v = term[q, :, cut] + precv[q, :, cut].astype(jnp.float32)
-            if not start:
-                ring_copy(s - 1, u, d).wait_recv()
-                v = v + rrecv[(s - 1) * SUBS + u, d].astype(jnp.float32)
-            v = v.astype(jnp.bfloat16)
-            if end:
-                ybuf[:, pl.ds(column(d, ring_chunk(n - 1, d), u), sub)] = v
-                gather_copy(0, u, d).start()
-                out_copy(n - 1, u, d).start()
-            else:
-                rsend[q, d] = v
-                ring_copy(s, u, d).start()
+        for h in range(HALVES):
+            for d in range(2):
+                p = u * HALVES + h
+                cut = slice(d * sub + h * piece, d * sub + (h + 1) * piece)
+                v = term[q, :, cut] + precv[q, :, cut].astype(jnp.float32)
+                if not start:
+                    ring_copy(s - 1, p, d).wait_recv()
+                    v = v + rrecv[(s - 1) * pieces + p, d].astype(jnp.float32)
+                v = v.astype(jnp.bfloat16)
+                if end:
+                    ybuf[place(ring_chunk(n - 1, d), p, d)] = v
+                    gather_copy(0, p, d).start()
+                else:
+                    rsend[s * pieces + p, d] = v
+                    ring_copy(s, p, d).start()
 
     def step(s, behind):
         for u in range(SUBS):
@@ -201,24 +218,33 @@
         pass_on(n - 1, u)
 
     for a in range(n - 1):
-        for u in range(SUBS):
+        for p in range(pieces):
             for d in range(2):
-                gather_copy(a, u, d).wait_recv()
+                gather_copy(a, p, d).wait_recv()
                 if a + 1 < n - 1:
-                    gather_copy(a + 1, u, d).start()
-                out_copy(a, u, d).start()
+                    gather_copy(a + 1, p, d).start()
 
     for i in range(slabs):
         partner_copy(i).wait_send()
     for q in range(pairs):
         term_copy(q).wait_send()
-    for a in range(n):
-        for u in range(SUBS):
+    for a in range(n - 1):
+        for p in range(pieces):
             for d in range(2):
-                if a < n - 1:
-                    ring_copy(a, u, d).wait_send()
-                    gather_copy(a, u, d).wait_send()
-                out_copy(a, u, d).wait()
+                ring_copy(a, p, d).wait_send()
+                gather_copy(a, p, d).wait_send()
+
+
+def lay_out(blocks, y_hbm, sem):
+    count, _, piece = blocks.shape
+    copies = [
+        pltpu.make_async_copy(blocks.at[i], y_hbm.at[:, pl.ds(i * piece, piece)], sem.at[i])
+        for i in range(count)
+    ]
+    for copy in copies:
+        copy.start()
+    for copy in copies:
+        copy.wait()
 
 
 def block(n, x, w_gate, w_up, w_down):
@@ -229,13 +255,16 @@
     slab = depth // SLABS
     sub = depth // (2 * n * SUBS)
     pairs = n * SUBS
+    pieces = SUBS * HALVES
+    piece = sub // HALVES
     bf16, f32 = jnp.bfloat16, jnp.float32
     dma = pltpu.SemaphoreType.DMA
-    return pl.pallas_call(
+    ring = (n - 1) * pieces
+    blocks = pl.pallas_call(
         functools.partial(kernel, n),
-        out_shape=jax.ShapeDtypeStruct((rows, depth), bf16),
+        out_shape=pltpu.VMEM((2 * n * pieces, rows, piece), bf16),
         in_specs=[pl.BlockSpec(memory_space=pl.ANY)] * 4,
-        out_specs=pl.BlockSpec(memory_space=pl.ANY),
+        out_specs=pl.BlockSpec(memory_space=pltpu.VMEM),
         scratch_shapes=[
             pltpu.VMEM((SLABS, 2 * rows, slab), bf16),
             pltpu.VMEM((2 * rows, 2 * width), f32),
@@ -245,20 +274,26 @@
             pltpu.VMEM((pairs, rows, 2 * sub), f32),
             pltpu.VMEM((pairs, rows, 2 * sub), bf16),
             pltpu.VMEM((pairs, rows, 2 * sub), bf16),
-            pltpu.VMEM((pairs - SUBS, 2, rows, sub), bf16),
-            pltpu.VMEM((pairs - SUBS, 2, rows, sub), bf16),
-            pltpu.VMEM((rows, depth), bf16),
+            pltpu.VMEM((ring, 2, rows, piece), bf16),
+            pltpu.VMEM((ring, 2, rows, piece), bf16),
             dma((SLABS,)), dma((SLABS,)), dma((SLABS,)),
-            dma((SLAB_SLOTS, 2)), dma((DOWN_SLOTS, 2)),
+            dma((SLAB_SLOTS, 2)), dma((PARTS, 2)), dma((DOWN_SLOTS, 2)),
             dma((pairs,)), dma((pairs,)),
-            dma((pairs - SUBS, 2)), dma((pairs - SUBS, 2)),
-            dma((pairs - SUBS, 2)), dma((pairs - SUBS, 2)),
-            dma((pairs, 2)),
+            dma((ring, 2)), dma((ring, 2)), dma((ring, 2)), dma((ring, 2)),
         ],
         compiler_params=pltpu.CompilerParams(
             collective_id=0, has_side_effects=True, vmem_limit_bytes=VMEM_BYTES),
         name="mlp",
     )(x, w_gate, w_up, w_down)
+    return pl.pallas_call(
+        lay_out,
+        out_shape=jax.ShapeDtypeStruct((rows, depth), bf16),
+        in_specs=[pl.BlockSpec(memory_space=pltpu.VMEM)],
+        out_specs=pl.BlockSpec(memory_space=pl.ANY),
+        scratch_shapes=[dma((2 * n * pieces,))],
+        compiler_params=pltpu.CompilerParams(vmem_limit_bytes=1 << 22),
+        name="lay_out",
+    )(blocks)
 
 
 def solution(mesh):

time: 115 us -> 113 us (0.983)
  local copies, waits for them, and re-layouts: 3.83 us -> 0 us
    unnamed x1 -> x0, local copies, waits for them, and re-layouts: 3.83 us -> none
    pallas_call x1 -> x2, Pallas kernels: 111 us -> 112 us  [the longest x1 110 us: block(): pl.pallas_call(functools.partial(kernel, n), out_shape=pltpu.VMEM((2 * n...]
where the time goes in v2:
time: 113 us
  Pallas kernels  112 us (99%)
    pallas_call x1, Pallas kernels, block(): pl.pallas_call(functools.partial(kernel, n), out_shape=pltpu.VMEM((2 * n...  110 us
    pallas_call x1, Pallas kernels, block(): pl.pallas_call(lay_out, out_shape=jax.ShapeDtypeStruct((rows, depth), bf1...  2.48 us

profile of v2, /device:TPU:21, one launch (start us, length us, event | category | flops | bytes accessed | tf_op | source)
XLA Modules:
  0.0 112.6 jit_solution(14994972825582624234)
XLA Ops:
  0.0 110.0 %mlp.1.blocks = bf16[96,128,128]{2,1,0:T(8,128)(2,1)S(1)} custom-call(bf16[128,12288]{1,0:T(8,128)(2,1)} %x_hbm.1, bf16[12288,4224]{1,0:T(8,128)(2,1)} %wg_hbm.1, bf16[12288,4224]{1,0:T(8,128)(2,1)} %wu_hbm.1, bf16[4224,12288]{1,0:T(8,128)(2,1)} %wd_hbm.1), custom_call_target="tpu_custom_call" | custom-call | tf_op jit(solution)/shard_map/mlp/pallas_call | solution.py:263
  110.0 2.5 %lay_out.1 = bf16[128,12288]{1,0:T(8,128)(2,1)} custom-call(bf16[96,128,128]{2,1,0:T(8,128)(2,1)S(1)} %mlp.1.blocks), custom_call_target="tpu_custom_call" | custom-call | tf_op jit(solution)/shard_map/lay_out/pallas_call | solution.py:288
